TPU v7x, 256 devices: a whole 4x4x8 slice. The times are simulated.
256 devices in a mesh: fsdp: 16 (over y, x), rep: 16 (over z, core).
Axes of the slice: x: 4, y: 4, z: 8, core: 2. Of those that a mesh axis runs over, the one named last changes fastest.
Arguments:
- gradient: float32 [11264, 8192], P('fsdp', 'rep'), may hold values from -6 to 6
- row_counts: int32 [16], replicated, may hold values from 1 to 704, 8192 in all
- owners: int32 [16, 16], P(None, 'rep'), may hold values from 0 to 15, as said below
- refresh_flags: int32 [16, 16], P(None, 'rep'), may hold values 0 or 1
- stat_left: float32 [16, 16, 512, 512], P('fsdp', 'rep'), as said below
- stat_right: float32 [16, 16, 512, 512], P('fsdp', 'rep'), as said below
- root_left: float32 [16, 16, 512, 512], P('fsdp', 'rep'), as said below
- root_right: float32 [16, 16, 512, 512], P('fsdp', 'rep'), as said below
Outputs:
- direction: bfloat16 [11264, 8192], P('fsdp')
- new_left: float32 [16, 16, 512, 512], P('fsdp', 'rep')
- new_right: float32 [16, 16, 512, 512], P('fsdp', 'rep')
Inputs may be any that keep to these rules, and one draw needn't show every extreme that they name: `owners`: in each column band of blocks every fsdp index owns exactly 1 block. `stat_left`: symmetric positive definite. `stat_right`: symmetric positive definite. `root_left`: symmetric positive definite. `root_right`: symmetric positive definite.
All inputs are finite; a program needn't handle non-finite values. No bound on the sum of `refresh_flags` on one device may be relied on, other than what follows from the above.
Results may differ from a plain program's by a relative error of at most 0.001.
Values may be sent and summed in bfloat16 or wider, within the bound.
No kernel may reach another device: no remote copies, remote signals or barrier semaphores. Data moves between devices by JAX's collectives and lax.ppermute only.
A program may use at most 128 MiB of HBM per device.

v0:
```python
import jax
import jax.numpy as jnp
from jax import lax
from jax.sharding import PartitionSpec as P

ITERS = 3
highest = lax.Precision.HIGHEST
stat_decay = 0.9
graft_eps = 1e-06


def matmul(left_part, right_part):
    return jnp.dot(left_part, right_part, precision=highest, preferred_element_type=jnp.float32)


def inverse_root(matrix, sweeps):
    identity = jnp.eye(matrix.shape[0], dtype=jnp.float32)
    scaling = 2.5 / jnp.sqrt(jnp.sum(matrix * matrix))
    current = identity * jnp.sqrt(jnp.sqrt(scaling))
    moment = matrix * scaling
    for sweep_pos in range(sweeps):
        factor = (5.0 * identity - moment) * 0.25
        current = matmul(current, factor)
        if sweep_pos + 1 < sweeps:
            squared = matmul(factor, factor)
            moment = matmul(matmul(squared, squared), moment)
    return current


def tile_update(grad_tile, left_stat, right_stat, old_left, old_right, refresh_now):
    fresh_left = stat_decay * left_stat + (1.0 - stat_decay) * matmul(grad_tile, grad_tile.T)
    fresh_right = stat_decay * right_stat + (1.0 - stat_decay) * matmul(grad_tile.T, grad_tile)
    left_root, right_root = lax.cond(
        refresh_now > 0,
        lambda: (inverse_root(fresh_left, ITERS), inverse_root(fresh_right, ITERS)),
        lambda: (old_left, old_right),
    )
    precond = matmul(matmul(left_root, grad_tile), right_root)
    graft_ratio = jnp.mean(grad_tile * grad_tile) / (jnp.mean(precond * precond) + graft_eps)
    return (fresh_left, fresh_right, (precond * jnp.sqrt(graft_ratio)).astype(jnp.bfloat16))


def slot_table(owners):
    band_count = owners.shape[0]
    same_owner = owners[:, None, :] == owners[None, :, :]
    ordinal = jnp.arange(band_count, dtype=jnp.int32)
    earlier = (ordinal[None, :] < ordinal[:, None])[:, :, None]
    return jnp.sum(jnp.where(same_owner & earlier, 1, 0), axis=1).astype(jnp.int32)


def flatten_blocks(values_in):
    return values_in.reshape((values_in.shape[0] * values_in.shape[1],) + values_in.shape[2:])


def update_items(block_items):
    return tile_update(*block_items)


def per_device(
    gradient, row_counts, owners, refresh_flags, stat_left, stat_right, root_left, root_right
):
    tile_size = stat_left.shape[-1]
    owner_index = lax.axis_index("fsdp")
    capacity, slab_width = gradient.shape
    band_count, columns = owners.shape
    slot_count = stat_left.shape[0]
    offsets = jnp.cumsum(row_counts) - row_counts
    slot_rank = slot_table(owners)
    holder = owners * slot_count + slot_rank
    band_ids = jnp.arange(band_count, dtype=jnp.int32)
    column_ids = jnp.arange(columns, dtype=jnp.int32)
    band_at = jnp.sum(
        jnp.where(holder[None, :, :] == band_ids[:, None, None], band_ids[None, :, None], 0), axis=1
    )
    my_bands = lax.dynamic_slice_in_dim(band_at, owner_index * slot_count, slot_count, 0)
    refresh_now = refresh_flags[my_bands, column_ids[None, :]]
    everything = lax.all_gather(gradient, "fsdp", axis=0, tiled=True)
    global_rows = my_bands[:, :, None] * tile_size + jnp.arange(tile_size, dtype=jnp.int32)
    source_index = jnp.sum((offsets <= global_rows[..., None]).astype(jnp.int32), axis=-1) - 1
    flat_index = source_index * capacity + global_rows - offsets[source_index]
    picked = jnp.take(everything, flat_index.reshape(-1), axis=0)
    picked = picked.reshape(slot_count, columns, tile_size, columns, tile_size)
    owned_tiles = picked[:, column_ids, :, column_ids, :].transpose(1, 0, 2, 3)
    fresh_lefts, fresh_rights, tile_stack = lax.map(
        update_items,
        (
            flatten_blocks(owned_tiles),
            flatten_blocks(stat_left),
            flatten_blocks(stat_right),
            flatten_blocks(root_left),
            flatten_blocks(root_right),
            refresh_now.reshape(-1),
        ),
    )
    new_left = fresh_lefts.reshape(stat_left.shape)
    new_right = fresh_rights.reshape(stat_right.shape)
    directions = tile_stack.reshape(slot_count, columns, tile_size, tile_size)
    gathered = lax.all_gather(directions, "fsdp", axis=0, tiled=True)
    local_rows = jnp.arange(capacity, dtype=jnp.int32)
    global_rows = offsets[owner_index] + local_rows
    live_rows = local_rows < row_counts[owner_index]
    band_pos = jnp.clip(global_rows // tile_size, 0, band_count - 1)
    within = global_rows % tile_size
    source_index = holder[band_pos]
    picked = gathered[source_index, column_ids[None, :], within[:, None]]
    row_slab = picked.reshape(capacity, slab_width)
    row_slab = jnp.where(live_rows[:, None], row_slab, jnp.zeros_like(row_slab))
    direction = lax.all_gather(row_slab, "rep", axis=1, tiled=True)
    return (direction, new_left, new_right)


def solution(mesh):
    return jax.shard_map(
        per_device,
        mesh=mesh,
        in_specs=(
            P("fsdp", "rep"),
            P(),
            P(None, "rep"),
            P(None, "rep"),
            P("fsdp", "rep", None, None),
            P("fsdp", "rep", None, None),
            P("fsdp", "rep", None, None),
            P("fsdp", "rep", None, None),
        ),
        out_specs=(P("fsdp", None), P("fsdp", "rep", None, None), P("fsdp", "rep", None, None)),
        check_vma=False,
    )
```

profile of v0, /device:TPU:1, one launch (start us, length us, event | category | flops | bytes accessed | tf_op | source)
XLA Modules:
  0.0 415.1 jit_solution(14211889260037414535)
XLA Ops:
  7.2 0.0 all-gather.5.cloned.1.call-start
  7.2 0.7 all-gather.5.cloned.1.call-update
  7.9 0.0 all-gather.9.cloned.1.call-start
  8.0 0.9 select_reduce_fusion.1
  8.9 0.7 bitcast_add_fusion
  9.5 0.1 select_reduce_fusion
  9.7 0.6 dynamic-slice.3
  12.8 0.1 add_bitcast_fusion.1
  12.9 1.3 fusion.111
  14.8 0.7 copy.17
  15.6 0.1 reduce.3
  15.7 0.7 sub.50
  16.4 0.7 fusion.110
  17.1 0.1 convert_reduce_fusion
  17.2 4.3 %compare_select_fusion.13 = (s32[1,1,512,1]{2,3,1,0:T(1,128)S(1)}, s32[1,1,512,1]{2,3,1,0:T(1,128)S(1)}) fusion(s32[]{:T(128)} %bitcast.25, s32[]{:T(128)} %bitcast.26, s32[]{:T(128)} %bitcast.27, s32[]{:T(128)} %bitcast.28, s32[]{:T(128)} %bitcast.29, s32[]{:T(128)} %bitcast.31, s32[]{:T(128)} %bitcast.30, s32[1,1,512,1]{2,3,1,0:T(1,128)S(1)} %bitcast.118, ...), kind=kLoop, calls=%fused_computation.147 | loop fusion | flops 7168 | bytes 8220 | tf_op jit(solution)/shard_map/gather | solution.py:80
  21.5 0.1 compare_reduce_fusion.17
  21.6 5.7 %compare_and_fusion = (pred[512]{0:T(512)(128)(4,1)S(1)}, s32[512]{0:T(512)S(1)}) fusion(s32[]{:T(128)} %bitcast.13, s32[512]{0:T(512)S(1)} %convert_reduce_fusion, pred[512]{0:T(512)(128)(4,1)S(1)} %get-tuple-element.76, pred[512]{0:T(512)(128)(4,1)S(1)} %get-tuple-element.75, pred[512]{0:T(512)(128)(4,1)S(1)} %get-tuple-element.74, ...), kind=kLoop, calls=%fused_computation.173 | loop fusion | flops 10240 | bytes 11304 | tf_op jit(solution)/shard_map/jit(_take)/and | solution.py:81
  27.3 135.2 %all-gather.5.cloned.1.call-done = f32[11264,512]{1,0:T(8,128)} async-done(((f32[704,512]{1,0:T(8,128)}), f32[11264,512]{1,0:T(8,128)}) %all-gather.5.cloned.1.call-update) | async-done | bytes 23068688 | tf_op jit(solution)/shard_map/all_gather | solution.py:77
  162.5 9.6 %gather_fusion = f32[512,512]{1,0:T(8,128)S(1)} fusion(f32[11264,512]{1,0:T(8,128)} %all-gather.5.cloned.1.call-done, s32[1024]{0:T(1024)S(1)} %pad_clamp_fusion), kind=kCustom, calls=%fused_computation | custom fusion | bytes 2099200 | tf_op jit(solution)/shard_map/jit(_take)/gather | solution.py:81
  172.1 1.0 fusion.90
  173.1 4.4 %fusion.84 = f32[512,512]{1,0:T(8,128)} fusion(f32[1,1,512,512]{3,2,1,0:T(8,128)} %param.15, f32[512,512]{1,0:T(8,128)S(1)} %gather_fusion, pred[512]{0:T(512)(128)(4,1)S(1)} %get-tuple-element.77), kind=kOutput, calls=%fused_computation.88 | convolution fusion | flops 1611661312 | bytes 3146240 | tf_op jit(solution)/shard_map/while/body/eval_jaxpr/dot_general | solution.py:13
  177.5 4.2 %fusion.85 = f32[512,512]{1,0:T(8,128)} fusion(f32[1,1,512,512]{3,2,1,0:T(8,128)} %param.14, f32[512,512]{1,0:T(8,128)S(1)} %gather_fusion, pred[512]{0:T(512)(128)(4,1)S(1)} %get-tuple-element.77), kind=kOutput, calls=%fused_computation.90 | convolution fusion | flops 1611661312 | bytes 3146240 | tf_op jit(solution)/shard_map/while/body/eval_jaxpr/dot_general | solution.py:13
  181.8 47.2 %conditional.1 = (f32[512,512]{1,0:T(8,128)S(1)}, f32[512,512]{1,0:T(8,128)S(1)}) conditional(s32[]{:T(128)} %bitcast.10, (f32[1,1,512,512]{3,2,1,0:T(8,128)S(1)}, f32[1,1,512,512]{3,2,1,0:T(8,128)S(1)}) %tuple.88, (f32[512,512]{1,0:T(8,128)}, f32[512,512]{1,0:T(8,128)}) %tuple.20), branch_computations={%region_4.5_spmd, %region_5.8_spmd} | conditional | flops 29005185024 | bytes 48234624 | solution.py:33
  182.2 2.4 multiply_reduce_fusion
  186.1 3.1 fusion.6
  189.2 3.1 fusion.8
  192.3 3.6 fusion.22
  195.9 1.8 fusion.115
  197.7 3.1 fusion.10
  200.8 1.9 fusion.16
  202.7 2.3 fusion.14
  205.1 1.8 fusion.116
  206.9 1.8 fusion.1
  208.8 1.8 fusion.117
  210.6 3.6 fusion.25
  214.3 1.8 fusion.112
  216.1 3.1 fusion.12
  219.2 2.1 fusion.20
  221.3 1.9 fusion.18
  223.2 1.8 fusion.113
  225.1 1.9 fusion
  226.9 1.8 fusion.114
  229.0 3.0 fusion.86
  232.7 3.9 multiply_reduce_fusion.2
  237.4 0.9 multiply_convert_fusion
  238.3 0.0 all-gather.9.cloned.1.call-update
  238.3 0.0 all-gather.7.cloned.1.call-start
  238.3 0.6 dynamic_slice.23
  238.9 0.7 compare_reduce_fusion.8
  239.6 0.7 compare_reduce_fusion.2
  240.3 0.7 compare_reduce_fusion.6
  241.0 0.7 compare_reduce_fusion.4
  241.7 0.7 compare_reduce_fusion
  242.4 0.7 fusion.109
  243.1 5.0 %fusion.98 = s32[704]{0:T(1024)S(1)} fusion(s32[]{:T(128)} %bitcast.51, s32[]{:T(128)} %bitcast.52, s32[]{:T(128)} %bitcast.53, s32[]{:T(128)} %bitcast.54, s32[]{:T(128)} %bitcast.55, s32[]{:T(128)} %bitcast.57, s32[]{:T(128)} %bitcast.56, s32[]{:T(128)} %bitcast.41), kind=kLoop, calls=%fused_computation.160 | loop fusion | flops 22528 | bytes 2848 | tf_op jit(solution)/shard_map/gather | solution.py:104
  248.1 0.6 iota_compare_fusion.5
  248.7 0.7 compare_select_fusion
  249.3 5.6 %select_select_fusion = s32[704]{0:T(1024)S(1)} fusion(pred[704]{0:T(1024)(128)(4,1)S(1)} %get-tuple-element.121, pred[704]{0:T(1024)(128)(4,1)S(1)} %get-tuple-element.122, pred[704]{0:T(1024)(128)(4,1)S(1)} %get-tuple-element.123, pred[704]{0:T(1024)(128)(4,1)S(1)} %get-tuple-element.124, pred[704]{0:T(1024)(128)(4,1)S(1)} %get-tuple-element.125, ...), kind=kLoop, calls=%fused_computation.158 | loop fusion | flops 6336 | bytes 12004 | tf_op jit(solution)/shard_map/gather | solution.py:104
  255.0 59.0 %all-gather.9.cloned.1.call-done = bf16[8192,512]{1,0:T(8,128)(2,1)} async-done(((bf16[512,512]{1,0:T(8,128)(2,1)}), bf16[8192,512]{1,0:T(8,128)(2,1)}) %all-gather.9.cloned.1.call-update) | async-done | bytes 8388624 | tf_op jit(solution)/shard_map/all_gather | solution.py:98
  314.0 12.1 %gather_fusion.1 = bf16[704,512]{1,0:T(8,128)(2,1)S(1)} fusion(bf16[16,1,512,512]{3,2,1,0:T(8,128)(2,1)} %bitcast.114, s32[704]{0:T(1024)S(1)} %fusion.105), kind=kCustom, calls=%fused_computation.1 | custom fusion | bytes 1450240 | tf_op jit(solution)/shard_map/gather | solution.py:105
  326.1 1.0 broadcast_select_fusion
  327.2 0.0 all-gather.7.cloned.1.call-update
  327.2 71.1 %all-gather.7.cloned.1.call-done = bf16[704,8192]{1,0:T(8,128)(2,1)} async-done(((bf16[704,512]{1,0:T(8,128)(2,1)}), bf16[704,8192]{1,0:T(8,128)(2,1)}) %all-gather.7.cloned.1.call-update) | async-done | bytes 11534352 | tf_op jit(solution)/shard_map/all_gather | solution.py:108
  398.3 10.0 %copy.30 = bf16[704,8192]{1,0:T(8,128)(2,1)} copy(bf16[704,8192]{1,0:T(8,128)(2,1)} %all-gather.7.cloned.1.call-done) | data formatting | bytes 23068672
  (15 shorter events, 0.1 us)
Async XLA Ops:
  7.2 174.6 %copy-start = (f32[1,1,512,512]{3,2,1,0:T(8,128)S(1)}, f32[1,1,512,512]{3,2,1,0:T(8,128)}, u32[]{:S(2)}) copy-start(f32[1,1,512,512]{3,2,1,0:T(8,128)} %param.16) | copy-start | bytes 3145732
  7.2 174.6 %copy-start.1 = (f32[1,1,512,512]{3,2,1,0:T(8,128)S(1)}, f32[1,1,512,512]{3,2,1,0:T(8,128)}, u32[]{:S(2)}) copy-start(f32[1,1,512,512]{3,2,1,0:T(8,128)} %param.17) | copy-start | bytes 3145732
  7.2 155.3 %all-gather.5.cloned.1.call-start = ((), (), s32[]{:S(2)}) async-start(), calls=%async_computation | async-start | bytes 24510464 | tf_op jit(solution)/shard_map/all_gather | solution.py:77
  7.9 306.1 %all-gather.9.cloned.1.call-start = ((), (), s32[]{:S(2)}) async-start(), calls=%async_computation.2 | async-start | bytes 8912896 | tf_op jit(solution)/shard_map/all_gather | solution.py:98
  181.8 56.6 %copy-start.2 = (s32[16]{0:T(128)S(1)}, s32[16]{0:T(128)}, u32[]{:S(2)}) copy-start(s32[16]{0:T(128)} %param.11) | copy-start | bytes 196
  238.3 160.0 %all-gather.7.cloned.1.call-start = ((), (), s32[]{:S(2)}) async-start(), calls=%async_computation.1 | async-start | bytes 12255232 | tf_op jit(solution)/shard_map/all_gather | solution.py:108
Sparse Core Ops, SparseCore 0:
  10.4 152.0 all-gather.4
  238.4 75.5 all-gather.8
  327.3 70.9 all-gather.6
where the time goes:
time: 421 us; the launch traced here: 415 us
  waiting for transfers between devices  266 us (63%)
  matrix products  58.1 us (14%)
  local copies, waits for them, and re-layouts  35.1 us (8%)
  other arithmetic  34.8 us (8%)
  between operations  18.8 us (4%)
    all_gather x1, waiting for transfers between devices, per_device(): everything = lax.all_gather(gradient, 'fsdp', axis=0, tiled=True)  135 us
    all_gather x1, waiting for transfers between devices, per_device(): direction = lax.all_gather(row_slab, 'rep', axis=1, tiled=True)  71.1 us
    all_gather x1, waiting for transfers between devices, per_device(): gathered = lax.all_gather(directions, 'fsdp', axis=0, tiled=True)  59 us
    dot_general x22, matrix products, matmul(): jnp.dot(left_part, right_part, precision=highest, preferred_element_type=...  58.1 us
    gather x7, other arithmetic, per_device(): source_index = holder[band_pos]  14.1 us
    gather x1, local copies, waits for them, and re-layouts, per_device(): picked = gathered[source_index, column_ids[None, :], within[:, None]]  12.1 us
    unnamed x7, local copies, waits for them, and re-layouts  10 us
    gather x1, local copies, waits for them, and re-layouts, per_device(): picked = jnp.take(everything, flat_index.reshape(-1), axis=0)  9.59 us
  transfers between devices with their start and end apart: 3, of which 3 were waited for; matrix products, arithmetic and copies ran while one was open for 8% of the time, Pallas kernels for 0%

commit v1 on v0

--- a/solution.py
+++ b/solution.py
@@ -95,7 +95,9 @@
     new_left = fresh_lefts.reshape(stat_left.shape)
     new_right = fresh_rights.reshape(stat_right.shape)
     directions = tile_stack.reshape(slot_count, columns, tile_size, tile_size)
-    gathered = lax.all_gather(directions, "fsdp", axis=0, tiled=True)
+    gathered = jnp.concatenate(
+        lax.all_to_all(jnp.stack([directions] * lax.axis_size("fsdp")), "fsdp", 0, 0), axis=0
+    )
     local_rows = jnp.arange(capacity, dtype=jnp.int32)
     global_rows = offsets[owner_index] + local_rows
     live_rows = local_rows < row_counts[owner_index]

time: 421 us -> 478 us (1.14)
  waiting for transfers between devices: 266 us -> 315 us
  starting transfers between devices: 0.12 us -> 5.17 us
    all_to_all x0 -> x1, waiting for transfers between devices: none -> 106 us  [per_device(): lax.all_to_all(jnp.stack([directions] * lax.axis_size('fsdp')), 'fsdp', 0...]
    all_gather x1 -> x0, waiting for transfers between devices: 59 us -> none  [per_device(): gathered = lax.all_gather(directions, 'fsdp', axis=0, tiled=True)]
    all_to_all x0 -> x1, starting transfers between devices: none -> 5.09 us  [per_device(): lax.all_to_all(jnp.stack([directions] * lax.axis_size('fsdp')), 'fsdp', 0...]
  transfers between devices with their start and end apart: 3 -> 3, of which waited for: 3 -> 3; matrix products, arithmetic and copies ran while one was open for 8% -> 7% of each run, Pallas kernels for 0% -> 0%
where the time goes in v1:
time: 478 us; the launch traced here: 473 us
  waiting for transfers between devices  315 us (66%)
  matrix products  58.1 us (12%)
  local copies, waits for them, and re-layouts  39.3 us (8%)
  other arithmetic  34 us (7%)
  between operations  19.2 us (4%)
  starting transfers between devices  5.17 us (1%)
    all_gather x1, waiting for transfers between devices, per_device(): everything = lax.all_gather(gradient, 'fsdp', axis=0, tiled=True)  135 us
    all_to_all x1, waiting for transfers between devices, per_device(): lax.all_to_all(jnp.stack([directions] * lax.axis_size('fsdp')), 'fsdp', 0...  106 us
    all_gather x1, waiting for transfers between devices, per_device(): direction = lax.all_gather(row_slab, 'rep', axis=1, tiled=True)  72.9 us
    dot_general x22, matrix products, matmul(): jnp.dot(left_part, right_part, precision=highest, preferred_element_type=...  58.1 us
    gather x7, other arithmetic, per_device(): source_index = holder[band_pos]  14.1 us
    gather x1, local copies, waits for them, and re-layouts, per_device(): picked = gathered[source_index, column_ids[None, :], within[:, None]]  12.1 us
    unnamed x7, local copies, waits for them, and re-layouts  10 us
    gather x1, local copies, waits for them, and re-layouts, per_device(): picked = jnp.take(everything, flat_index.reshape(-1), axis=0)  9.59 us
  transfers between devices with their start and end apart: 3, of which 3 were waited for; matrix products, arithmetic and copies ran while one was open for 7% of the time, Pallas kernels for 0%

profile of v1, /device:TPU:1, one launch (start us, length us, event | category | flops | bytes accessed | tf_op | source)
XLA Modules:
  0.0 472.6 jit_solution(4706428350036857776)
XLA Ops:
  7.2 0.0 all-gather.3.cloned.1.call-start
  7.2 0.7 all-gather.3.cloned.1.call-update
  7.9 0.9 select_reduce_fusion.1
  8.8 0.7 bitcast_add_fusion
  9.5 0.1 select_reduce_fusion
  9.6 0.6 dynamic-slice.3
  12.8 0.1 add_bitcast_fusion.1
  12.9 1.3 fusion.111
  14.8 0.7 copy.16
  15.6 0.1 reduce.3
  15.7 0.7 sub.50
  16.4 0.7 fusion.110
  17.1 0.1 convert_reduce_fusion
  17.2 4.3 compare_select_fusion.13
  21.5 0.1 compare_reduce_fusion.17
  21.6 5.7 %compare_and_fusion = (pred[512]{0:T(512)(128)(4,1)S(1)}, s32[512]{0:T(512)S(1)}) fusion(s32[]{:T(128)} %bitcast.13, s32[512]{0:T(512)S(1)} %convert_reduce_fusion, pred[512]{0:T(512)(128)(4,1)S(1)} %get-tuple-element.76, pred[512]{0:T(512)(128)(4,1)S(1)} %get-tuple-element.75, pred[512]{0:T(512)(128)(4,1)S(1)} %get-tuple-element.74, ...), kind=kLoop, calls=%fused_computation.173 | loop fusion | flops 10240 | bytes 11304 | tf_op jit(solution)/shard_map/jit(_take)/and | solution.py:81
  27.3 135.2 %all-gather.3.cloned.1.call-done = f32[11264,512]{1,0:T(8,128)} async-done(((f32[704,512]{1,0:T(8,128)}), f32[11264,512]{1,0:T(8,128)}) %all-gather.3.cloned.1.call-update) | async-done | bytes 23068688 | tf_op jit(solution)/shard_map/all_gather | solution.py:77
  162.5 9.6 %gather_fusion = f32[512,512]{1,0:T(8,128)S(1)} fusion(f32[11264,512]{1,0:T(8,128)} %all-gather.3.cloned.1.call-done, s32[1024]{0:T(1024)S(1)} %pad_clamp_fusion), kind=kCustom, calls=%fused_computation | custom fusion | bytes 2099200 | tf_op jit(solution)/shard_map/jit(_take)/gather | solution.py:81
  172.1 1.0 fusion.90
  173.1 4.4 fusion.84
  177.5 4.2 fusion.85
  181.8 46.8 %conditional.1 = (f32[512,512]{1,0:T(8,128)S(1)}, f32[512,512]{1,0:T(8,128)S(1)}) conditional(s32[]{:T(128)} %bitcast.10, (f32[1,1,512,512]{3,2,1,0:T(8,128)S(1)}, f32[1,1,512,512]{3,2,1,0:T(8,128)S(1)}) %tuple.86, (f32[512,512]{1,0:T(8,128)}, f32[512,512]{1,0:T(8,128)}) %tuple.20), branch_computations={%region_4.5_spmd, %region_5.8_spmd} | conditional | flops 29005185024 | bytes 48234624 | solution.py:33
  181.8 2.4 multiply_reduce_fusion
  185.6 3.1 fusion.6
  188.8 3.1 fusion.8
  191.9 3.6 fusion.22
  195.5 1.8 fusion.115
  197.3 3.1 fusion.10
  200.4 1.9 fusion.16
  202.3 2.3 fusion.14
  204.7 1.8 fusion.116
  206.5 1.9 fusion.1
  208.4 1.8 fusion.117
  210.2 3.6 fusion.25
  213.9 1.8 fusion.112
  215.7 3.1 fusion.12
  218.8 2.1 fusion.20
  220.9 1.9 fusion.18
  222.8 1.8 fusion.113
  224.7 1.9 fusion
  226.5 1.8 fusion.114
  228.6 3.0 fusion.86
  232.3 3.9 multiply_reduce_fusion.2
  236.9 0.1 multiply_convert_fusion
  237.1 4.2 stack.3
  241.3 5.1 %all-to-all-start = ((bf16[16,1,1,512,512]{4,3,2,1,0:T(8,128)(2,1)}), bf16[16,1,1,512,512]{4,3,2,1,0:T(8,128)(2,1)}, u32[]{:S(2)}, u32[]{:S(2)}) async-start(bf16[16,1,1,512,512]{4,3,2,1,0:T(8,128)(2,1)} %stack.3), calls=%async_computation | async-start | bytes 16777216 | tf_op jit(solution)/shard_map/all_to_all | solution.py:99
  246.4 0.0 all-gather.5.cloned.1.call-start
  246.5 0.6 dynamic_slice.23
  247.0 0.7 compare_reduce_fusion.8
  247.7 0.7 compare_reduce_fusion.2
  248.4 0.7 compare_reduce_fusion.6
  249.1 0.7 compare_reduce_fusion.4
  249.8 0.7 compare_reduce_fusion
  250.5 0.7 fusion.109
  251.2 5.0 %fusion.98 = s32[704]{0:T(1024)S(1)} fusion(s32[]{:T(128)} %bitcast.50, s32[]{:T(128)} %bitcast.51, s32[]{:T(128)} %bitcast.52, s32[]{:T(128)} %bitcast.53, s32[]{:T(128)} %bitcast.54, s32[]{:T(128)} %bitcast.56, s32[]{:T(128)} %bitcast.55, s32[]{:T(128)} %bitcast.40), kind=kLoop, calls=%fused_computation.160 | loop fusion | flops 22528 | bytes 2848 | tf_op jit(solution)/shard_map/gather | solution.py:106
  256.2 0.6 iota_compare_fusion.5
  256.8 0.7 compare_select_fusion
  257.5 5.6 %select_select_fusion = s32[704]{0:T(1024)S(1)} fusion(pred[704]{0:T(1024)(128)(4,1)S(1)} %get-tuple-element.121, pred[704]{0:T(1024)(128)(4,1)S(1)} %get-tuple-element.122, pred[704]{0:T(1024)(128)(4,1)S(1)} %get-tuple-element.123, pred[704]{0:T(1024)(128)(4,1)S(1)} %get-tuple-element.124, pred[704]{0:T(1024)(128)(4,1)S(1)} %get-tuple-element.125, ...), kind=kLoop, calls=%fused_computation.158 | loop fusion | flops 6336 | bytes 12004 | tf_op jit(solution)/shard_map/gather | solution.py:106
  263.1 106.3 %all-to-all-done = bf16[16,1,1,512,512]{4,3,2,1,0:T(8,128)(2,1)} async-done(((bf16[16,1,1,512,512]{4,3,2,1,0:T(8,128)(2,1)}), bf16[16,1,1,512,512]{4,3,2,1,0:T(8,128)(2,1)}, u32[]{:S(2)}, u32[]{:S(2)}) %all-to-all-start) | async-done | bytes 8388640 | tf_op jit(solution)/shard_map/all_to_all | solution.py:99
  369.5 12.1 %gather_fusion.1 = bf16[704,512]{1,0:T(8,128)(2,1)S(1)} fusion(bf16[16,1,512,512]{3,2,1,0:T(8,128)(2,1)} %bitcast.39, s32[704]{0:T(1024)S(1)} %fusion.105), kind=kCustom, calls=%fused_computation.1 | custom fusion | bytes 1450240 | tf_op jit(solution)/shard_map/gather | solution.py:107
  381.6 1.0 broadcast_select_fusion
  382.6 0.0 all-gather.5.cloned.1.call-update
  382.7 72.9 %all-gather.5.cloned.1.call-done = bf16[704,8192]{1,0:T(8,128)(2,1)} async-done(((bf16[704,512]{1,0:T(8,128)(2,1)}), bf16[704,8192]{1,0:T(8,128)(2,1)}) %all-gather.5.cloned.1.call-update) | async-done | bytes 11534352 | tf_op jit(solution)/shard_map/all_gather | solution.py:110
  455.5 10.0 %copy.28 = bf16[704,8192]{1,0:T(8,128)(2,1)} copy(bf16[704,8192]{1,0:T(8,128)(2,1)} %all-gather.5.cloned.1.call-done) | data formatting | bytes 23068672
  (15 shorter events, 0.1 us)
Async XLA Ops:
  7.2 174.6 %copy-start = (f32[1,1,512,512]{3,2,1,0:T(8,128)S(1)}, f32[1,1,512,512]{3,2,1,0:T(8,128)}, u32[]{:S(2)}) copy-start(f32[1,1,512,512]{3,2,1,0:T(8,128)} %param.16) | copy-start | bytes 3145732
  7.2 174.6 %copy-start.1 = (f32[1,1,512,512]{3,2,1,0:T(8,128)S(1)}, f32[1,1,512,512]{3,2,1,0:T(8,128)}, u32[]{:S(2)}) copy-start(f32[1,1,512,512]{3,2,1,0:T(8,128)} %param.17) | copy-start | bytes 3145732
  7.2 155.3 %all-gather.3.cloned.1.call-start = ((), (), s32[]{:S(2)}) async-start(), calls=%async_computation.1 | async-start | bytes 24510464 | tf_op jit(solution)/shard_map/all_gather | solution.py:77
  237.1 9.4 %copy-start.2 = (s32[16]{0:T(128)S(1)}, s32[16]{0:T(128)}, u32[]{:S(2)}) copy-start(s32[16]{0:T(128)} %param.11) | copy-start | bytes 196
  241.3 128.2 %all-to-all-start = ((bf16[16,1,1,512,512]{4,3,2,1,0:T(8,128)(2,1)}), bf16[16,1,1,512,512]{4,3,2,1,0:T(8,128)(2,1)}, u32[]{:S(2)}, u32[]{:S(2)}) async-start(bf16[16,1,1,512,512]{4,3,2,1,0:T(8,128)(2,1)} %stack.3), calls=%async_computation | async-start | bytes 16777216 | tf_op jit(solution)/shard_map/all_to_all | solution.py:99
  246.4 209.1 %all-gather.5.cloned.1.call-start = ((), (), s32[]{:S(2)}) async-start(), calls=%async_computation.2 | async-start | bytes 12255232 | tf_op jit(solution)/shard_map/all_gather | solution.py:110
Sparse Core Ops, SparseCore 0:
  10.4 151.9 all-gather.2
  382.8 72.6 all-gather.4
